TPU v7x, 128 devices: a whole 4x4x4 slice. The times are simulated.
128 devices in a mesh: rep: 4 (over x_hi, core), tp: 32 (over z, x_lo, y).
Axes of the slice: x: 4 (x_hi: 2, x_lo: 2; x = x_hi * 2 + x_lo), y: 4, z: 4, core: 2. Of those that a mesh axis runs over, the one named last changes fastest.
Arguments:
- trainer_query: float32 [128, 64, 8192], P(('rep', 'tp')), may hold values from -6 to 6
- trainer_output: float32 [128, 8192, 64], P(('rep', 'tp')), may hold values from -6 to 6
- probes: bfloat16 [768, 8192], replicated, may hold values from -0.0625 to 0.0625
- shard_block: int32 [128], replicated, may hold values from 0 to 127, each once
- slice_owner: int32 [32], replicated, may hold values from 0 to 31, each once
Outputs:
- query_slices: bfloat16 [32, 8192, 256], P('tp')
- output_slices: bfloat16 [32, 256, 8192], P('tp')
- query_prints: float32 [32, 768, 256], P('tp')
- output_prints: float32 [32, 256, 768], P('tp')
Inputs may be any that keep to these rules, and one draw needn't show every extreme that they name: `shard_block`: a permutation: each number once. `slice_owner`: a permutation: each number once.
All inputs are finite; a program needn't handle non-finite values.
Results may differ from a plain program's by a relative error of at most 0.0029.
Values may be sent and summed in bfloat16 or wider, within the bound.
A program may use at most 128 MiB of HBM per device.

v0:
```python
import jax
import jax.numpy as jnp
from jax import lax
from jax.sharding import PartitionSpec as P


def cut_along(shard, dim, length):
    dims = shard.shape
    pieces = shard.reshape(*dims[:dim], length, dims[dim] // length, *dims[dim + 1 :])
    return jnp.moveaxis(pieces, dim, 0)


def edges_of(length, count):
    unit = 8 if length >= 8 * count else 1
    return [length // unit * k // count * unit for k in range(1, count)]


def laid_out(pieces, dim):
    pieces = jnp.moveaxis(pieces, 0, dim)
    dims = pieces.shape
    return pieces.reshape(*dims[:dim], dims[dim] * dims[dim + 1], *dims[dim + 2 :])


def cut_exchange(shard, axis, pieces, split_dim, concat_dim):
    blocks = cut_along(shard, split_dim, lax.axis_size(axis))
    split_at = max(range(1, max(2, blocks.ndim - 1)), key=lambda d: blocks.shape[d])
    outs = []
    for section in jnp.split(blocks, edges_of(blocks.shape[split_at], pieces), axis=split_at):
        if section.size:
            outs.append(lax.all_to_all(section, axis, split_axis=0, concat_axis=0, tiled=True))
    return laid_out(jnp.concatenate(outs, axis=split_at), concat_dim)


def per_device(trainer_query, trainer_output, probes, shard_block, slice_owner):
    tp_count = lax.axis_size("tp")
    rep_count = lax.axis_size("rep")
    dev_count = tp_count * rep_count
    shard_rows = trainer_query.shape[1]
    query_width = trainer_query.shape[2]
    slice_width = query_width // tp_count
    model_width = shard_rows * dev_count
    positions = jnp.arange(dev_count, dtype=jnp.int32)
    inverse = jnp.zeros((dev_count,), jnp.int32).at[shard_block].set(positions)
    query_local = trainer_query[0].astype(jnp.bfloat16)
    query_blocks = jnp.take(
        query_local.reshape(shard_rows, tp_count, slice_width), slice_owner, axis=1
    ).reshape(shard_rows, query_width)
    output_local = trainer_output[0].astype(jnp.bfloat16)
    output_blocks = jnp.take(
        output_local.reshape(tp_count, slice_width, shard_rows), slice_owner, axis=0
    ).reshape(query_width, shard_rows)
    query_moved = lax.all_to_all(query_blocks, "tp", split_axis=1, concat_axis=0, tiled=True)
    query_all = lax.all_gather(query_moved, "rep", axis=0, tiled=True)
    output_moved = cut_exchange(output_blocks, "tp", 2, 0, 1)
    output_all = lax.all_gather(output_moved, "rep", axis=1, tiled=True)
    query_ordered = query_all.reshape(dev_count, shard_rows, slice_width)
    query_slice = jnp.take(query_ordered, inverse, axis=0).reshape(model_width, slice_width)
    output_ordered = output_all.reshape(slice_width, dev_count, shard_rows)
    output_slice = jnp.take(output_ordered, inverse, axis=1).reshape(slice_width, model_width)
    query_prints = jnp.dot(probes, query_slice, preferred_element_type=jnp.float32)
    output_prints = lax.dot_general(
        output_slice, probes, (((1,), (1,)), ((), ())), preferred_element_type=jnp.float32
    )
    return (query_slice[None], output_slice[None], query_prints[None], output_prints[None])


def solution(mesh):
    placed = (P(("rep", "tp"), None, None), P(("rep", "tp"), None, None), P(), P(), P())
    return jax.shard_map(
        per_device,
        mesh=mesh,
        in_specs=placed,
        out_specs=(
            P("tp", None, None),
            P("tp", None, None),
            P("tp", None, None),
            P("tp", None, None),
        ),
        check_vma=False,
    )
```

profile of v0, /device:TPU:1, one launch (start us, length us, event | category | flops | bytes accessed | tf_op | source)
XLA Modules:
  0.0 165.8 jit_solution(11763954619681203649)
XLA Ops:
  7.2 0.7 compare_select_fusion
  7.9 0.7 compare_and_fusion
  8.5 1.7 %convert_element_type.16 = bf16[1,8192,64]{1,2,0:T(8,128)(2,1)S(1)} convert(f32[1,8192,64]{1,2,0:T(8,128)} %param.6) | non-fusion elementwise | flops 524288 | bytes 3145728 | tf_op jit(solution)/shard_map/convert_element_type | solution.py:48
  10.2 0.3 copy.17
  10.5 0.6 copy.13
  11.1 0.6 gather_fusion.2
  11.7 0.2 broadcast_select_fusion
  11.9 0.3 fusion.2
  12.2 19.7 %all_to_all.26 = bf16[32,128,64]{1,2,0:T(8,128)(2,1)S(1)} all-to-all(bf16[32,128,64]{1,2,0:T(8,128)(2,1)S(1)} %get-tuple-element.16), channel_id=1, replica_groups=mesh['rep'=4,'tp'=32] {'tp'}, dimensions={0} | all-to-all | bytes 1048576 | tf_op jit(solution)/shard_map/all_to_all | solution.py:30
  31.9 15.4 %all_to_all.27 = bf16[32,128,64]{1,2,0:T(8,128)(2,1)S(1)} all-to-all(bf16[32,128,64]{1,2,0:T(8,128)(2,1)S(1)} %get-tuple-element.17), channel_id=1, replica_groups=mesh['rep'=4,'tp'=32] {'tp'}, dimensions={0} | all-to-all | bytes 1048576 | tf_op jit(solution)/shard_map/all_to_all | solution.py:30
  47.2 1.1 pad_maximum_fusion
  48.4 0.1 convert_element_type.14
  48.6 0.3 copy.16
  48.8 0.6 copy.12
  49.4 0.6 gather_fusion
  50.0 0.2 select_bitcast_fusion
  50.2 27.8 %all_to_all.28 = bf16[64,32,256]{2,0,1:T(8,128)(2,1)} all-to-all(bf16[64,32,256]{2,0,1:T(8,128)(2,1)S(1)} %select_bitcast_fusion), channel_id=1, replica_groups=mesh['rep'=4,'tp'=32] {'tp'}, dimensions={1} | all-to-all | bytes 2097152 | tf_op jit(solution)/shard_map/all_to_all | solution.py:52
  78.1 1.2 scatter_custom_fusion
  79.3 0.1 broadcast_in_dim.66
  79.4 0.1 broadcast_in_dim.67
  79.5 15.6 %all-gather.5.cloned.1.call-done = bf16[256,8192]{0,1:T(8,128)(2,1)} async-done(((bf16[256,2048]{0,1:T(8,128)(2,1)}), bf16[256,8192]{0,1:T(8,128)(2,1)}) %all-gather.5.cloned.1.call-update) | async-done | bytes 4194320 | tf_op jit(solution)/shard_map/all_gather | solution.py:55
  95.1 5.0 %gather_fusion.3 = bf16[128,256,64]{1,2,0:T(8,128)(2,1)} fusion(bf16[256,128,64]{0,2,1:T(8,128)(2,1)} %bitcast.43, s32[1024]{0:T(1024)S(1)} %pad_clamp_fusion), kind=kCustom, calls=%fused_computation.3 | custom fusion | bytes 8389120 | tf_op jit(solution)/shard_map/jit(_take)/gather | solution.py:59
  100.1 5.3 %bitcast_select_fusion.1 = bf16[1,256,8192]{1,2,0:T(8,128)(2,1)} fusion(pred[8192]{0:T(1024)(128)(4,1)S(1)} %broadcast_in_dim.67, bf16[1,256,8192]{1,2,0:T(8,128)(2,1)} %bitcast.41), kind=kLoop, calls=%fused_computation.6 | loop fusion | flops 2097152 | bytes 8396800 | tf_op jit(solution)/shard_map/jit(_take)/select_n | solution.py:59
  105.3 6.5 %copy.14 = bf16[1,256,8192]{2,1,0:T(8,128)(2,1)} copy(bf16[1,256,8192]{1,2,0:T(8,128)(2,1)} %bitcast_select_fusion.1) | data formatting | bytes 8388608
  111.8 6.0 %bitcast_select_fusion = bf16[256,8192]{0,1:T(8,128)(2,1)S(1)} fusion(bf16[128,256,64]{1,2,0:T(8,128)(2,1)} %gather_fusion.3, pred[8192]{0:T(1024)(128)(4,1)S(1)} %broadcast_in_dim.67), kind=kLoop, calls=%fused_computation.5 | loop fusion | flops 2097152 | bytes 8396800 | tf_op jit(solution)/shard_map/jit(_take)/select_n | solution.py:59
  117.8 7.4 %convolution_bitcast_fusion = f32[1,256,768]{2,1,0:T(8,128)} fusion(bf16[256,8192]{0,1:T(8,128)(2,1)S(1)} %bitcast_select_fusion, bf16[768,8192]{1,0:T(8,128)(2,1)} %param.7), kind=kOutput, calls=%fused_computation.9 | convolution fusion | flops 3221225472 | bytes 17563648 | tf_op jit(solution)/shard_map/dot_general | solution.py:61
  125.2 9.8 %all-gather.3.cloned.1.call-done = bf16[8192,256]{1,0:T(8,128)(2,1)} async-done(((bf16[2048,256]{1,0:T(8,128)(2,1)}), bf16[8192,256]{1,0:T(8,128)(2,1)}) %all-gather.3.cloned.1.call-update) | async-done | bytes 4194320 | tf_op jit(solution)/shard_map/all_gather | solution.py:53
  135.0 5.0 %gather_fusion.1 = bf16[128,64,256]{2,1,0:T(8,128)(2,1)} fusion(bf16[128,64,256]{2,1,0:T(8,128)(2,1)} %bitcast.46, s32[1024]{0:T(1024)S(1)} %pad_clamp_fusion), kind=kCustom, calls=%fused_computation.1 | custom fusion | bytes 8389120 | tf_op jit(solution)/shard_map/jit(_take)/gather | solution.py:57
  140.1 6.0 %bitcast_select_fusion.2 = bf16[8192,256]{1,0:T(8,128)(2,1)S(1)} fusion(bf16[128,64,256]{2,1,0:T(8,128)(2,1)} %gather_fusion.1, pred[8192]{0:T(1024)(128)(4,1)S(1)} %broadcast_in_dim.67), kind=kLoop, calls=%fused_computation.7 | loop fusion | flops 2097152 | bytes 8396800 | tf_op jit(solution)/shard_map/jit(_take)/select_n | solution.py:57
  146.0 6.5 %convolution_bitcast_fusion.1 = f32[1,768,256]{1,2,0:T(8,128)S(1)} fusion(bf16[8192,256]{1,0:T(8,128)(2,1)S(1)} %bitcast_select_fusion.2, bf16[768,8192]{1,0:T(8,128)(2,1)} %param.7), kind=kOutput, calls=%fused_computation.10 | convolution fusion | flops 3221225472 | bytes 17563648 | tf_op jit(solution)/shard_map/dot_general | solution.py:60
  152.6 1.1 copy.15
  153.7 5.2 %bitcast_select_fusion.3 = bf16[1,8192,256]{2,1,0:T(8,128)(2,1)} fusion(pred[8192]{0:T(1024)(128)(4,1)S(1)} %broadcast_in_dim.67, bf16[1,8192,256]{2,1,0:T(8,128)(2,1)} %bitcast.42), kind=kLoop, calls=%fused_computation.8 | loop fusion | flops 2097152 | bytes 8396800 | tf_op jit(solution)/shard_map/jit(_take)/select_n | solution.py:57
  (14 shorter events, 0.2 us)
Async XLA Ops:
  7.2 87.9 %all-gather.5.cloned.1.call-start = ((), (), s32[]{:S(2)}) async-start(), calls=%async_computation.4 | async-start | bytes 5242880 | tf_op jit(solution)/shard_map/all_gather | solution.py:55
  11.9 36.5 %copy-start = (f32[1,64,8192]{2,1,0:T(8,128)S(1)}, f32[1,64,8192]{2,1,0:T(8,128)}, u32[]{:S(2)}) copy-start(f32[1,64,8192]{2,1,0:T(8,128)} %param.5) | copy-start | bytes 6291460
  48.4 86.7 %all-gather.3.cloned.1.call-start = ((), (), s32[]{:S(2)}) async-start(), calls=%async_computation.3 | async-start | bytes 5242880 | tf_op jit(solution)/shard_map/all_gather | solution.py:53
  49.4 28.7 %copy-start.1 = (s32[128]{0:T(128)S(1)}, s32[128]{0:T(128)}, u32[]{:S(2)}) copy-start(s32[128]{0:T(128)} %param.8) | copy-start | bytes 1540
Sparse Core Ops, SparseCore 0:
  48.5 46.5 all-gather.4
  96.7 38.2 all-gather.2
where the time goes:
time: 167 us; the launch traced here: 166 us
  blocking collectives  62.9 us (38%)
  other arithmetic  27 us (16%)
  waiting for transfers between devices  25.4 us (15%)
  local copies, waits for them, and re-layouts  22.2 us (13%)
  between operations  14.2 us (9%)
  matrix products  13.9 us (8%)
    all_to_all x2, blocking collectives, cut_exchange(): lax.all_to_all(section, axis, split_axis=0, concat_axis=0, tiled=True)  35 us
    all_to_all x1, blocking collectives, per_device(): lax.all_to_all(query_blocks, 'tp', split_axis=1, concat_axis=0, tiled=True)  27.8 us
    all_gather x1, waiting for transfers between devices, per_device(): output_all = lax.all_gather(output_moved, 'rep', axis=1, tiled=True)  15.6 us
    select_n x2, other arithmetic, per_device(): jnp.take(output_ordered, inverse, axis=1).reshape(slice_width, model_width)  11.2 us
    select_n x3, other arithmetic, per_device(): jnp.take(query_ordered, inverse, axis=0).reshape(model_width, slice_width)  11.2 us
    all_gather x1, waiting for transfers between devices, per_device(): query_all = lax.all_gather(query_moved, 'rep', axis=0, tiled=True)  9.84 us
    unnamed x8, local copies, waits for them, and re-layouts  8.14 us
    dot_general x1, matrix products, per_device(): lax.dot_general(output_slice, probes, (((1,), (1,)), ((), ())), preferred...  7.43 us
  transfers between devices with their start and end apart: 2, of which 2 were waited for; matrix products, arithmetic and copies ran while one was open for 20% of the time, Pallas kernels for 0%

commit v1 on v0

v1 whole, which is shorter than its diff:
```python
import jax
import jax.numpy as jnp
from jax import lax
from jax.experimental import pallas as pl
from jax.experimental.pallas import tpu as pltpu
from jax.sharding import PartitionSpec as P

MESH = pl.DeviceIdType.MESH
BF16 = jnp.bfloat16
F32 = jnp.float32

ROUNDS = 16
LAG_X = 3
LAG_D = 4


def near_first(i):
    return lax.rem(lax.div(i * (i + 1), 2), 4)


def offset_of(k):
    k = jnp.int32(k)
    return near_first(lax.rem(k, 4)), near_first(lax.div(k, 4))


def place():
    rep, tp = lax.axis_index("rep"), lax.axis_index("tp")
    x = lax.div(rep, 2) * 2 + lax.rem(lax.div(tp, 4), 2)
    return x, lax.rem(tp, 4), lax.div(tp, 8), lax.rem(rep, 2)


def device(x, y, z, core):
    x, y, z = lax.rem(x, 4), lax.rem(y, 4), lax.rem(z, 4)
    return {"rep": lax.div(x, 2) * 2 + core, "tp": z * 8 + lax.rem(x, 2) * 4 + y}


def move_kernel(
    owner, block, query, output, probes,
    recv, turned, prints,
    query_f, output_f, probes_v, staged, relay, lhs, rhs,
    load_sem, probe_sem, near_s, near_r, far_s, far_r, x_s, x_r, d_s, d_r,
):
    x, y, z, core = place()
    mine = z * 4 + y
    barrier = pltpu.get_barrier_semaphore()
    peers = [device(x, y + k % 4, z + k // 4, core) for k in range(1, ROUNDS)]
    peers += [device(x + d, y, z, core) for d in (1, 2, 3)] + [device(x, y, z, 1 - core)]

    def load(kind, i):
        if kind == 2:
            cols = pl.ds(pl.multiple_of(i * 128, 128), 128)
            return pltpu.make_async_copy(probes.at[:, cols], probes_v.at[i], probe_sem.at[i])
        cols = pl.ds(pl.multiple_of(i * 256, 256), 256)
        src, dst = ((query, query_f), (output, output_f))[kind]
        return pltpu.make_async_copy(src.at[:, cols], dst.at[i], load_sem.at[kind, i])

    @pl.loop(0, 32)
    def _(i):
        load(0, i).start()
        load(1, i).start()

    @pl.loop(0, 64)
    def _(i):
        load(2, i).start()

    for peer in peers:
        pl.semaphore_signal(barrier, 1, device_id=peer, device_id_type=MESH)

    def remote(src, dst, send, receive, target):
        return pltpu.make_async_remote_copy(
            src_ref=src, dst_ref=dst, send_sem=send, recv_sem=receive,
            device_id=target, device_id_type=MESH,
        )

    def plane_of(k):
        dy, dz = offset_of(k)
        return lax.rem(z - dz + 4, 4) * 4 + lax.rem(y - dy + 4, 4)

    def near(k):
        dy, dz = offset_of(k)
        return remote(staged.at[k, 0], recv.at[mine, core, x], near_s.at[k], near_r.at[k],
                      device(x, y + dy, z + dz, core))

    def far(k):
        dy, dz = offset_of(k)
        return remote(staged.at[k, 1], relay.at[k], far_s.at[k], far_r.at[k],
                      device(x, y + dy, z + dz, core))

    def along(k):
        own = recv.at[plane_of(k), core, x]
        return (
            remote(relay.at[k], own, x_s.at[k, 0], x_r.at[k, 0], device(x + 1, y, z, core)),
            remote(relay.at[k], own, x_s.at[k, 1], x_r.at[k, 1], device(x + 3, y, z, core)),
            remote(own, own, x_s.at[k, 2], x_r.at[k, 2], device(x + 2, y, z, core)),
        )

    def across(k):
        half = recv.at[plane_of(k), core]
        return remote(half, half, d_s.at[k], d_r.at[k], device(x, y, z, 1 - core))

    def piece(k, other):
        dy, dz = offset_of(k)
        low = lax.rem(x + other, 2)
        j = lax.rem(z + dz, 4) * 8 + low * 4 + lax.rem(y + dy, 4)
        at = owner[j]
        return query_f[at].astype(BF16), output_f[at].astype(BF16)

    @pl.loop(0, 32)
    def _(i):
        load(0, i).wait()
        load(1, i).wait()

    recv[mine, core, x, 0:64, :], recv[mine, core, x, 64:128, :] = piece(0, 0)
    relay[0, 0:64, :], relay[0, 64:128, :] = piece(0, 1)

    def stage(k):
        for other in (0, 1):
            staged[k, other, 0:64, :], staged[k, other, 64:128, :] = piece(k, other)

    stage(1)
    pl.semaphore_wait(barrier, len(peers))
    for copy in along(0):
        copy.start()

    @pl.loop(2, ROUNDS + 1)
    def _(k):
        @pl.when(k < ROUNDS)
        def _():
            stage(k)

        far(k - 1).start()
        near(k - 1).start()

    prints[...] = jnp.zeros_like(prints)

    @pl.loop(0, 64)
    def _(i):
        load(2, i).wait()

    half = lax.div(lax.broadcasted_iota(jnp.int32, (128, 256), 0), 64)

    def compute(k):
        plane = plane_of(k)
        src_z, src_y = lax.div(plane, 4), lax.rem(plane, 4)
        for i in range(8):
            src_c, src_x = i // 4, i % 4
            shard = ((src_x // 2) * 2 + src_c) * 32 + src_z * 8 + (src_x % 2) * 4 + src_y
            at = block[shard]
            lhs[:, i * 128 : (i + 1) * 128] = probes_v[lax.div(at, 2)]
            q = recv[plane, src_c, src_x, 0:64, :]
            o = recv[plane, src_c, src_x, 64:128, :]
            held = half == lax.rem(at, 2)
            for part, data in enumerate((q, o)):
                pair = jnp.concatenate([data, data], axis=0)
                cols = slice(part * 256, (part + 1) * 256)
                rhs[i * 128 : (i + 1) * 128, cols] = jnp.where(held, pair, jnp.zeros_like(pair))
            turned[plane * 8 + i] = jnp.concatenate([o, o], axis=0).T

        @pl.loop(0, 3)
        def _(m):
            rows = pl.ds(pl.multiple_of(m * 256, 256), 256)
            prints[rows, :] += jnp.dot(lhs[rows, :], rhs[...], preferred_element_type=F32)

    @pl.loop(0, ROUNDS + LAG_D)
    def _(t):
        @pl.when((t >= 1) & (t < ROUNDS))
        def _():
            far(t).wait_recv()
            first, second, third = along(t)
            first.start()
            second.start()
            near(t).wait_recv()
            third.start()

        @pl.when((t >= LAG_X) & (t < ROUNDS + LAG_X))
        def _():
            for copy in along(t - LAG_X):
                copy.wait_recv()
            across(t - LAG_X).start()

        @pl.when(t >= LAG_D)
        def _():
            across(t - LAG_D).wait_recv()
            compute(t - LAG_D)

    @pl.loop(0, ROUNDS)
    def _(k):
        @pl.when(k >= 1)
        def _():
            near(k).wait_send()
            far(k).wait_send()

        for copy in along(k):
            copy.wait_send()
        across(k).wait_send()


def place_kernel(block, recv, turned, prints, q_out, o_out, qp_out, op_out,
                 slot_of, o_all, op_all, sems):
    qp = pltpu.make_async_copy(prints.at[:, 0:256], qp_out, sems.at[1])
    qp.start()

    @pl.loop(0, 128)
    def _(g):
        plane, src_c, src_x = g // 8, (g // 4) % 2, g % 4
        shard = ((src_x // 2) * 2 + src_c) * 32 + (plane // 4) * 8 + (src_x % 2) * 4 + plane % 4
        at = block[shard]
        slot_of[at] = g
        pltpu.make_async_copy(
            recv.at[plane, src_c, src_x, 0:64, :], q_out.at[pl.ds(pl.multiple_of(at * 64, 64), 64), :], sems.at[0]
        ).start()

    left = lax.broadcasted_iota(jnp.int32, (256, 128), 1) < 64
    outs = []
    for part in range(4):
        @pl.loop(part * 16, (part + 1) * 16)
        def _(p):
            one = turned[slot_of[2 * p]]
            two = turned[slot_of[2 * p + 1]]
            o_all[:, pl.ds(pl.multiple_of(p * 128, 128), 128)] = jnp.where(left, one, two)

        cols = slice(part * 2048, (part + 1) * 2048)
        copy = pltpu.make_async_copy(o_all.at[:, cols], o_out.at[:, cols], sems.at[3 + part])
        copy.start()
        outs.append(copy)
    op_all[...] = prints[:, 256:512].T
    op = pltpu.make_async_copy(op_all, op_out, sems.at[2])
    op.start()
    for copy in [qp, op] + outs:
        copy.wait()
    pltpu.make_async_copy(q_out, q_out, sems.at[0]).wait()


def per_device(trainer_query, trainer_output, probes, shard_block, slice_owner):
    smem = pl.BlockSpec(memory_space=pltpu.SMEM)
    hbm = pl.BlockSpec(memory_space=pl.ANY)
    vmem = pl.BlockSpec(memory_space=pltpu.VMEM)
    dma = pltpu.SemaphoreType.DMA
    recv, turned, prints = pl.pallas_call(
        move_kernel,
        out_shape=(
            pltpu.VMEM((16, 2, 4, 128, 256), BF16),
            pltpu.VMEM((128, 256, 128), BF16),
            pltpu.VMEM((768, 512), F32),
        ),
        in_specs=[smem, smem, hbm, hbm, hbm],
        out_specs=(vmem, vmem, vmem),
        scratch_shapes=[
            pltpu.VMEM((32, 64, 256), F32),
            pltpu.VMEM((32, 64, 256), F32),
            pltpu.VMEM((64, 768, 128), BF16),
            pltpu.VMEM((ROUNDS, 2, 128, 256), BF16),
            pltpu.VMEM((ROUNDS, 128, 256), BF16),
            pltpu.VMEM((768, 1024), BF16),
            pltpu.VMEM((1024, 512), BF16),
            dma((2, 32)), dma((64,)), dma((ROUNDS,)), dma((ROUNDS,)), dma((ROUNDS,)), dma((ROUNDS,)),
            dma((ROUNDS, 3)), dma((ROUNDS, 3)), dma((ROUNDS,)), dma((ROUNDS,)),
        ],
        compiler_params=pltpu.CompilerParams(
            collective_id=0, has_side_effects=True, vmem_limit_bytes=44 << 20
        ),
        name="move",
    )(
        slice_owner, shard_block, trainer_query[0], jnp.swapaxes(trainer_output, 1, 2)[0], probes
    )
    outs = pl.pallas_call(
        place_kernel,
        out_shape=(
            jax.ShapeDtypeStruct((8192, 256), BF16),
            jax.ShapeDtypeStruct((256, 8192), BF16),
            jax.ShapeDtypeStruct((768, 256), F32),
            jax.ShapeDtypeStruct((256, 768), F32),
        ),
        in_specs=[smem, vmem, vmem, vmem],
        out_specs=(hbm, hbm, hbm, hbm),
        scratch_shapes=[
            pltpu.SMEM((128,), jnp.int32),
            pltpu.VMEM((256, 8192), BF16),
            pltpu.VMEM((256, 768), F32),
            dma((8,)),
        ],
        compiler_params=pltpu.CompilerParams(vmem_limit_bytes=32 << 20),
        name="place",
    )(shard_block, recv, turned, prints)
    return tuple(out[None] for out in outs)


def solution(mesh):
    placed = (P(("rep", "tp"), None, None), P(("rep", "tp"), None, None), P(), P(), P())
    return jax.shard_map(
        per_device,
        mesh=mesh,
        in_specs=placed,
        out_specs=(
            P("tp", None, None),
            P("tp", None, None),
            P("tp", None, None),
            P("tp", None, None),
        ),
        check_vma=False,
    )
```

time: 167 us -> 80.2 us (0.48)
  Pallas kernels: 0 us -> 72.7 us
  blocking collectives: 62.9 us -> 0 us
  other arithmetic: 27 us -> 0 us
  waiting for transfers between devices: 25.4 us -> 0 us
  local copies, waits for them, and re-layouts: 22.2 us -> 6.59 us
  matrix products: 13.9 us -> 0 us
  between operations: 14.2 us -> 0.66 us
    pallas_call x0 -> x2, Pallas kernels: none -> 72.7 us  [the longest x1 65 us: per_device(): pl.pallas_call(move_kernel, out_shape=(pltpu.VMEM((16, 2, 4, 128, 256), B...]
    all_to_all x3 -> x0, blocking collectives: 62.9 us -> none  [the longest x2 35 us: cut_exchange(): lax.all_to_all(section, axis, split_axis=0, concat_axis=0, tiled=True)]
    all_gather x2 -> x0, waiting for transfers between devices: 25.4 us -> none  [the longest x1 15.6 us: per_device(): output_all = lax.all_gather(output_moved, 'rep', axis=1, tiled=True)]
    select_n x9 -> x0, other arithmetic: 23.4 us -> none  [the longest x2 11.2 us: per_device(): jnp.take(output_ordered, inverse, axis=1).reshape(slice_width, model_width)]
    dot_general x2 -> x0, matrix products: 13.9 us -> none  [the longest x1 7.43 us: per_device(): lax.dot_general(output_slice, probes, (((1,), (1,)), ((), ())), preferred...]
    gather x4 -> x0, local copies, waits for them, and re-layouts: 11.3 us -> none  [the longest x1 5.01 us: per_device(): jnp.take(output_ordered, inverse, axis=1).reshape(slice_width, model_width)]
    convert_element_type x2 -> x0, other arithmetic: 1.8 us -> none  [the longest x1 1.7 us: per_device(): output_local = trainer_output[0].astype(jnp.bfloat16)]
    unnamed x8 -> x6, local copies, waits for them, and re-layouts: 8.14 us -> 6.59 us
  transfers between devices with their start and end apart: 2 -> 0, of which waited for: 2 -> 0; matrix products, arithmetic and copies ran while one was open for 20% -> 0% of each run, Pallas kernels for 0% -> 0%
where the time goes in v1:
time: 80.2 us; the launch traced here: 80 us
  Pallas kernels  72.7 us (91%)
  local copies, waits for them, and re-layouts  6.59 us (8%)
    pallas_call x1, Pallas kernels, per_device(): pl.pallas_call(move_kernel, out_shape=(pltpu.VMEM((16, 2, 4, 128, 256), B...  65 us
    pallas_call x1, Pallas kernels, per_device(): pl.pallas_call(place_kernel, out_shape=(jax.ShapeDtypeStruct((8192, 256),...  7.77 us
    unnamed x6, local copies, waits for them, and re-layouts  6.59 us

profile of v1, /device:TPU:1, one launch (start us, length us, event | category | flops | bytes accessed | tf_op | source)
XLA Modules:
  0.0 80.0 jit_solution(8020601459364192880)
XLA Ops:
  0.6 0.0 copy-start.2
  0.6 65.0 %move.1 = (bf16[16,2,4,128,256]{4,3,2,1,0:T(8,128)(2,1)S(1)}, bf16[128,256,128]{2,1,0:T(8,128)(2,1)S(1)}, f32[768,512]{1,0:T(8,128)S(1)}) custom-call(s32[32]{0:T(128)} %owner.1, s32[128]{0:T(128)} %block.3, f32[64,8192]{1,0:T(8,128)} %bitcast.8, f32[64,8192]{1,0:T(8,128)} %bitcast.9, bf16[768,8192]{1,0:T(8,128)(2,1)} %probes.1), custom_call_target="tpu_custom_call" | custom-call | tf_op jit(solution)/shard_map/move/pallas_call | solution.py:239
  65.6 0.0 copy-start
  65.6 3.2 %copy-done = bf16[16,2,4,128,256]{4,3,2,1,0:T(8,128)(2,1)} copy-done((bf16[16,2,4,128,256]{4,3,2,1,0:T(8,128)(2,1)}, bf16[16,2,4,128,256]{4,3,2,1,0:T(8,128)(2,1)S(1)}, u32[]{:S(2)}) %copy-start) | copy-done | bytes 8388632
  68.8 0.0 copy-done.2
  68.8 0.0 copy-start.1
  68.8 3.4 %copy-done.1 = bf16[16,2,4,128,256]{4,3,2,1,0:T(8,128)(2,1)S(1)} copy-done((bf16[16,2,4,128,256]{4,3,2,1,0:T(8,128)(2,1)S(1)}, bf16[16,2,4,128,256]{4,3,2,1,0:T(8,128)(2,1)}, u32[]{:S(2)}) %copy-start.1) | copy-done | bytes 8388632
  72.2 7.8 %place.1 = (bf16[8192,256]{1,0:T(8,128)(2,1)}, bf16[256,8192]{1,0:T(8,128)(2,1)}, f32[768,256]{1,0:T(8,128)}, f32[256,768]{1,0:T(8,128)}) custom-call(s32[128]{0:T(128)S(1)} %copy-done.2, bf16[16,2,4,128,256]{4,3,2,1,0:T(8,128)(2,1)S(1)} %copy-done.1, bf16[128,256,128]{2,1,0:T(8,128)(2,1)S(1)} %get-tuple-element.12.turned, ...), custom_call_target="tpu_custom_call" | custom-call | tf_op jit(solution)/shard_map/place/pallas_call | solution.py:266
Async XLA Ops:
  0.6 68.2 %copy-start.2 = (s32[128]{0:T(128)S(1)}, s32[128]{0:T(128)}, u32[]{:S(2)}) copy-start(s32[128]{0:T(128)} %block.3) | copy-start | bytes 1540
  65.6 3.2 %copy-start = (bf16[16,2,4,128,256]{4,3,2,1,0:T(8,128)(2,1)}, bf16[16,2,4,128,256]{4,3,2,1,0:T(8,128)(2,1)S(1)}, u32[]{:S(2)}) copy-start(bf16[16,2,4,128,256]{4,3,2,1,0:T(8,128)(2,1)S(1)} %get-tuple-element.11.recv) | copy-start | bytes 25165828
  68.8 3.4 %copy-start.1 = (bf16[16,2,4,128,256]{4,3,2,1,0:T(8,128)(2,1)S(1)}, bf16[16,2,4,128,256]{4,3,2,1,0:T(8,128)(2,1)}, u32[]{:S(2)}) copy-start(bf16[16,2,4,128,256]{4,3,2,1,0:T(8,128)(2,1)} %copy-done) | copy-start | bytes 25165828

commit v2 on v1

v2 whole, which is shorter than its diff:
```python
import jax
import jax.numpy as jnp
from jax import lax
from jax.experimental import pallas as pl
from jax.experimental.pallas import tpu as pltpu
from jax.sharding import PartitionSpec as P

MESH = pl.DeviceIdType.MESH
BF16 = jnp.bfloat16
F32 = jnp.float32

ROUNDS = 16
LAG_X = 3
LAG_D = 4
DIRECT = 0


def near_first(i):
    return lax.rem(lax.div(i * (i + 1), 2), 4)


def offset_of(k):
    k = jnp.int32(k)
    return near_first(lax.rem(k, 4)), near_first(lax.div(k, 4))


def place():
    rep, tp = lax.axis_index("rep"), lax.axis_index("tp")
    x = lax.div(rep, 2) * 2 + lax.rem(lax.div(tp, 4), 2)
    return x, lax.rem(tp, 4), lax.div(tp, 8), lax.rem(rep, 2)


def device(x, y, z, core):
    x, y, z = lax.rem(x, 4), lax.rem(y, 4), lax.rem(z, 4)
    return {"rep": lax.div(x, 2) * 2 + core, "tp": z * 8 + lax.rem(x, 2) * 4 + y}


def move_kernel(
    owner, block, block_row, query, output, probes,
    recv, turned, prints, slot_of,
    query_f, output_f, probes_v, staged, relay, lhs, rhs,
    load_sem, probe_sem, near_s, near_r, far_s, far_r, x_s, x_r, d_s, d_r,
):
    x, y, z, core = place()
    mine = z * 4 + y
    barrier = pltpu.get_barrier_semaphore()
    peers = [device(x, y + k % 4, z + k // 4, core) for k in range(1, ROUNDS)]
    peers += [device(x + d, y, z, core) for d in (1, 2, 3)] + [device(x, y, z, 1 - core)]
    if DIRECT:
        peers += [device(x + d, y + 2, z + 2, core) for d in (1, 2, 3)]

    def load(kind, i):
        src, dst = ((query, query_f), (output, output_f))[kind]
        return pltpu.make_async_copy(src.at[i], dst.at[i], load_sem.at[kind, i])

    def load_probes(i):
        rows = pl.ds(i * 12, 12)
        return pltpu.make_async_copy(probes.at[rows], probes_v.at[rows], probe_sem.at[i])

    for i in range(8):
        load(0, i).start()
        load(1, i).start()
    for i in range(8):
        load_probes(i).start()
    for peer in peers:
        pl.semaphore_signal(barrier, 1, device_id=peer, device_id_type=MESH)

    def remote(src, dst, send, receive, target):
        return pltpu.make_async_remote_copy(
            src_ref=src, dst_ref=dst, send_sem=send, recv_sem=receive,
            device_id=target, device_id_type=MESH,
        )

    def plane_of(k):
        dy, dz = offset_of(k)
        return lax.rem(z - dz + 4, 4) * 4 + lax.rem(y - dy + 4, 4)

    def slot(plane, src_core, src_x):
        return plane * 8 + src_core * 4 + src_x

    def near(k):
        dy, dz = offset_of(k)
        return remote(staged.at[k, 0], recv.at[slot(mine, core, x)], near_s.at[k], near_r.at[k],
                      device(x, y + dy, z + dz, core))

    def far(k):
        dy, dz = offset_of(k)
        return remote(staged.at[k, 1], relay.at[k], far_s.at[k], far_r.at[k],
                      device(x, y + dy, z + dz, core))

    def along(k):
        own = recv.at[slot(plane_of(k), core, x)]
        return (
            remote(relay.at[k], own, x_s.at[k, 0], x_r.at[k, 0], device(x + 1, y, z, core)),
            remote(relay.at[k], own, x_s.at[k, 1], x_r.at[k, 1], device(x + 3, y, z, core)),
            remote(own, own, x_s.at[k, 2], x_r.at[k, 2], device(x + 2, y, z, core)),
        )

    def diagonal():
        k, own = ROUNDS - 1, recv.at[slot(mine, core, x)]
        return [
            remote(staged.at[k, other], own, x_s.at[k, i], x_r.at[k, i],
                   device(x + d, y + 2, z + 2, core))
            for i, (d, other) in enumerate(((1, 1), (3, 1), (2, 0)))
        ]

    def across(k):
        half = recv.at[pl.ds(slot(plane_of(k), core, 0), 4)]
        return remote(half, half, d_s.at[k], d_r.at[k], device(x, y, z, 1 - core))

    def piece(source, k, other, part):
        dy, dz = offset_of(k)
        low = lax.rem(x + other, 2)
        j = lax.rem(z + dz, 4) * 8 + low * 4 + lax.rem(y + dy, 4)
        return source[:, owner[j], part].reshape(64, 128).astype(BF16)

    def cut(dst, k, other):
        for row, source in ((0, query_f), (64, output_f)):
            for part in (0, 1):
                dst[row : row + 64, part * 128 : (part + 1) * 128] = piece(source, k, other, part)

    def stage(k):
        for other in (0, 1):
            cut(staged.at[k, other], k, other)

    for i in range(8):
        load(0, i).wait()
        load(1, i).wait()
    cut(recv.at[slot(mine, core, x)], 0, 0)
    cut(relay.at[0], 0, 1)
    if DIRECT:
        stage(ROUNDS - 1)
    stage(1)
    pl.semaphore_wait(barrier, len(peers))
    for copy in along(0):
        copy.start()
    far(1).start()
    near(1).start()
    if DIRECT:
        for copy in diagonal():
            copy.start()
    stage(2)

    @pl.loop(2, ROUNDS - DIRECT)
    def _(k):
        @pl.when(k < ROUNDS - 1 - DIRECT)
        def _():
            stage(k + 1)

        far(k).start()
        near(k).start()

    if DIRECT:
        near(ROUNDS - 1).start()

    prints[...] = jnp.zeros_like(prints)

    held_block = jnp.broadcast_to(block_row[...].astype(F32), (128, 128)).T
    shard = lax.broadcasted_iota(jnp.int32, (128, 128), 0)
    rep, tp = lax.div(shard, 32), lax.rem(shard, 32)
    src_x = lax.div(rep, 2) * 2 + lax.rem(lax.div(tp, 4), 2)
    where = slot(lax.div(tp, 8) * 4 + lax.rem(tp, 4), lax.rem(rep, 2), src_x)
    hit = held_block == lax.broadcasted_iota(jnp.int32, (128, 128), 1).astype(F32)
    slot_of[...] = jnp.sum(
        jnp.where(hit, where.astype(F32), 0.0), axis=0, keepdims=True
    ).astype(jnp.int32)

    half = lax.div(lax.broadcasted_iota(jnp.int32, (128, 256), 0), 64)

    def compute(k, src_core):
        plane = plane_of(k)
        src_z, src_y = lax.div(plane, 4), lax.rem(plane, 4)
        for src_x in range(4):
            shard = ((src_x // 2) * 2 + src_core) * 32 + src_z * 8 + (src_x % 2) * 4 + src_y
            at = block[shard]
            at_slot = slot(plane, src_core, src_x)
            lhs[:, src_x * 128 : (src_x + 1) * 128] = probes_v[:, lax.div(at, 2)].reshape(768, 128)
            q = recv[at_slot, 0:64, :]
            o = recv[at_slot, 64:128, :]
            held = half == lax.rem(at, 2)
            for part, data in enumerate((q, o)):
                pair = jnp.concatenate([data, data], axis=0)
                cols = slice(part * 256, (part + 1) * 256)
                rhs[src_x * 128 : (src_x + 1) * 128, cols] = jnp.where(
                    held, pair, jnp.zeros_like(pair)
                )
            turned[at_slot] = jnp.concatenate([o, o], axis=0).T

        @pl.loop(0, 3)
        def _(m):
            rows = pl.ds(pl.multiple_of(m * 256, 256), 256)
            prints[rows, :] += jnp.dot(lhs[rows, :], rhs[...], preferred_element_type=F32)

    @pl.loop(0, ROUNDS + LAG_D)
    def _(t):
        @pl.when((t >= 1) & (t < ROUNDS - DIRECT))
        def _():
            far(t).wait_recv()
            first, second, third = along(t)
            first.start()
            second.start()
            near(t).wait_recv()
            third.start()

        if DIRECT:
            @pl.when(t == ROUNDS - 1)
            def _():
                near(t).wait_recv()

        @pl.when((t >= LAG_X) & (t < ROUNDS + LAG_X))
        def _():
            for copy in along(t - LAG_X):
                copy.wait_recv()
            across(t - LAG_X).start()

            @pl.when(t == LAG_X)
            def _():
                for i in range(8):
                    load_probes(i).wait()

            compute(t - LAG_X, core)

        @pl.when(t >= LAG_D)
        def _():
            across(t - LAG_D).wait_recv()
            compute(t - LAG_D, 1 - core)

    @pl.loop(0, ROUNDS)
    def _(k):
        @pl.when(k >= 1)
        def _():
            near(k).wait_send()

        @pl.when((k >= 1) & (k < ROUNDS - DIRECT))
        def _():
            far(k).wait_send()

        for copy in along(k):
            copy.wait_send()
        across(k).wait_send()


def place_kernel(slot_of, recv, turned, prints, q_out, o_out, qp_out, op_out,
                 o_all, op_all, sems):
    qp = pltpu.make_async_copy(prints.at[:, 0:256], qp_out, sems.at[1])
    qp.start()
    left = lax.broadcasted_iota(jnp.int32, (256, 128), 1) < 64
    outs = []
    for part in range(4):
        @pl.loop(part * 16, (part + 1) * 16)
        def _(p):
            slots = slot_of[0, 2 * p], slot_of[0, 2 * p + 1]
            for i in (0, 1):
                rows = pl.ds(pl.multiple_of(p * 128 + i * 64, 64), 64)
                pltpu.make_async_copy(
                    recv.at[slots[i], 0:64, :], q_out.at[rows, :], sems.at[0]
                ).start()
            cols = pl.ds(pl.multiple_of(p * 128, 128), 128)
            o_all[:, cols] = jnp.where(left, turned[slots[0]], turned[slots[1]])

        cols = slice(part * 2048, (part + 1) * 2048)
        copy = pltpu.make_async_copy(o_all.at[:, cols], o_out.at[:, cols], sems.at[3 + part])
        copy.start()
        outs.append(copy)
    op_all[...] = prints[:, 256:512].T
    op = pltpu.make_async_copy(op_all, op_out, sems.at[2])
    op.start()
    for copy in [qp, op] + outs:
        copy.wait()
    pltpu.make_async_copy(q_out, q_out, sems.at[0]).wait()


def tiles(shard):
    return shard.reshape(8, 8, 32, 2, 128).transpose(0, 2, 3, 1, 4)


def per_device(trainer_query, trainer_output, probes, shard_block, slice_owner):
    smem = pl.BlockSpec(memory_space=pltpu.SMEM)
    hbm = pl.BlockSpec(memory_space=pltpu.HBM)
    vmem = pl.BlockSpec(memory_space=pltpu.VMEM)
    dma = pltpu.SemaphoreType.DMA

    def in_hbm(array):
        return pltpu.with_memory_space_constraint(array, pltpu.HBM)

    recv, turned, prints, slot_of = pl.pallas_call(
        move_kernel,
        out_shape=(
            pltpu.VMEM((128, 128, 256), BF16),
            pltpu.VMEM((128, 256, 128), BF16),
            pltpu.VMEM((768, 512), F32),
            pltpu.VMEM((1, 128), jnp.int32),
        ),
        in_specs=[smem, smem, vmem, hbm, hbm, hbm],
        out_specs=(vmem, vmem, vmem, vmem),
        scratch_shapes=[
            pltpu.VMEM((8, 32, 2, 8, 128), F32),
            pltpu.VMEM((8, 32, 2, 8, 128), F32),
            pltpu.VMEM((96, 64, 8, 128), BF16),
            pltpu.VMEM((ROUNDS, 2, 128, 256), BF16),
            pltpu.VMEM((ROUNDS, 128, 256), BF16),
            pltpu.VMEM((768, 512), BF16),
            pltpu.VMEM((512, 512), BF16),
            dma((2, 8)), dma((8,)), dma((ROUNDS,)), dma((ROUNDS,)), dma((ROUNDS,)), dma((ROUNDS,)),
            dma((ROUNDS, 3)), dma((ROUNDS, 3)), dma((ROUNDS,)), dma((ROUNDS,)),
        ],
        compiler_params=pltpu.CompilerParams(
            collective_id=0, has_side_effects=True, vmem_limit_bytes=30 << 20
        ),
        name="move",
    )(
        in_hbm(slice_owner),
        in_hbm(shard_block),
        in_hbm(shard_block.reshape(1, 128)),
        in_hbm(tiles(trainer_query[0])),
        in_hbm(tiles(jnp.swapaxes(trainer_output, 1, 2)[0])),
        in_hbm(probes.reshape(96, 8, 64, 128).transpose(0, 2, 1, 3)),
    )
    outs = pl.pallas_call(
        place_kernel,
        out_shape=(
            jax.ShapeDtypeStruct((8192, 256), BF16),
            jax.ShapeDtypeStruct((256, 8192), BF16),
            jax.ShapeDtypeStruct((768, 256), F32),
            jax.ShapeDtypeStruct((256, 768), F32),
        ),
        in_specs=[smem, vmem, vmem, vmem],
        out_specs=(hbm, hbm, hbm, hbm),
        scratch_shapes=[
            pltpu.VMEM((256, 8192), BF16),
            pltpu.VMEM((256, 768), F32),
            dma((8,)),
        ],
        compiler_params=pltpu.CompilerParams(vmem_limit_bytes=10 << 20),
        name="place",
    )(slot_of, recv, turned, prints)
    return tuple(out[None] for out in outs)


def solution(mesh):
    placed = (P(("rep", "tp"), None, None), P(("rep", "tp"), None, None), P(), P(), P())
    return jax.shard_map(
        per_device,
        mesh=mesh,
        in_specs=placed,
        out_specs=(
            P("tp", None, None),
            P("tp", None, None),
            P("tp", None, None),
            P("tp", None, None),
        ),
        check_vma=False,
    )
```

time: 80.2 us -> 71.2 us (0.89)
  local copies, waits for them, and re-layouts: 6.59 us -> 0 us
  Pallas kernels: 72.7 us -> 70.4 us
    unnamed x6 -> x0, local copies, waits for them, and re-layouts: 6.59 us -> none
    pallas_call x1, Pallas kernels: 7.77 us -> 4.36 us  [per_device(): pl.pallas_call(place_kernel, out_shape=(jax.ShapeDtypeStruct((8192, 256),...]
    pallas_call x1, Pallas kernels: 65 us -> 66 us  [per_device(): pl.pallas_call(move_kernel, out_shape=(pltpu.VMEM((128, 128, 256), BF16),...]
where the time goes in v2:
time: 71.2 us; the launch traced here: 71 us
  Pallas kernels  70.4 us (99%)
    pallas_call x1, Pallas kernels, per_device(): pl.pallas_call(move_kernel, out_shape=(pltpu.VMEM((128, 128, 256), BF16),...  66 us
    pallas_call x1, Pallas kernels, per_device(): pl.pallas_call(place_kernel, out_shape=(jax.ShapeDtypeStruct((8192, 256),...  4.36 us

profile of v2, /device:TPU:1, one launch (start us, length us, event | category | flops | bytes accessed | tf_op | source)
XLA Modules:
  0.0 71.0 jit_solution(15116857022588780745)
XLA Ops:
  0.6 66.0 %move.1 = (bf16[128,128,256]{2,1,0:T(8,128)(2,1)S(1)}, bf16[128,256,128]{2,1,0:T(8,128)(2,1)S(1)}, f32[768,512]{1,0:T(8,128)S(1)}, s32[1,128]{1,0:T(1,128)S(1)}) custom-call(s32[32]{0:T(128)} %owner.1, s32[128]{0:T(128)} %block.1, s32[1,128]{1,0:T(1,128)} %bitcast.19, f32[8,32,2,8,128]{4,3,2,1,0:T(8,128)} %bitcast.17, f32[8,32,2,8,128]{4,3,2,1,0:T(8,128)} %bitcast.18, ...), custom_call_target="tpu_custom_call" | custom-call | tf_op jit(solution)/shard_map/move/pallas_call | solution.py:286
  66.6 4.4 %place.1 = (bf16[8192,256]{1,0:T(8,128)(2,1)}, bf16[256,8192]{1,0:T(8,128)(2,1)}, f32[768,256]{1,0:T(8,128)}, f32[256,768]{1,0:T(8,128)}) custom-call(s32[1,128]{1,0:T(1,128)S(1)} %get-tuple-element.12.slot_of, bf16[128,128,256]{2,1,0:T(8,128)(2,1)S(1)} %get-tuple-element.13.recv, bf16[128,256,128]{2,1,0:T(8,128)(2,1)S(1)} %get-tuple-element.14.turned, ...), custom_call_target="tpu_custom_call" | custom-call | tf_op jit(solution)/shard_map/place/pallas_call | solution.py:319

commit v3 on v2

--- a/solution.py
+++ b/solution.py
@@ -13,6 +13,7 @@
 LAG_X = 3
 LAG_D = 4
 DIRECT = 0
+AHEAD = 4
 
 
 def near_first(i):
@@ -60,8 +61,6 @@
     for i in range(8):
         load(0, i).start()
         load(1, i).start()
-    for i in range(8):
-        load_probes(i).start()
     for peer in peers:
         pl.semaphore_signal(barrier, 1, device_id=peer, device_id_type=MESH)
 
@@ -139,20 +138,13 @@
     if DIRECT:
         for copy in diagonal():
             copy.start()
-    stage(2)
-
-    @pl.loop(2, ROUNDS - DIRECT)
-    def _(k):
-        @pl.when(k < ROUNDS - 1 - DIRECT)
-        def _():
-            stage(k + 1)
-
+    for k in range(2, AHEAD + 1):
+        stage(k)
         far(k).start()
         near(k).start()
 
-    if DIRECT:
-        near(ROUNDS - 1).start()
-
+    for i in range(8):
+        load_probes(i).start()
     prints[...] = jnp.zeros_like(prints)
 
     held_block = jnp.broadcast_to(block_row[...].astype(F32), (128, 128)).T
@@ -167,25 +159,32 @@
 
     half = lax.div(lax.broadcasted_iota(jnp.int32, (128, 256), 0), 64)
 
-    def compute(k, src_core):
+    lane_half = lax.div(lax.broadcasted_iota(jnp.int32, (768, 128), 1), 64)
+
+    def arrange(k, src_core, at_half):
         plane = plane_of(k)
         src_z, src_y = lax.div(plane, 4), lax.rem(plane, 4)
-        for src_x in range(4):
-            shard = ((src_x // 2) * 2 + src_core) * 32 + src_z * 8 + (src_x % 2) * 4 + src_y
-            at = block[shard]
-            at_slot = slot(plane, src_core, src_x)
-            lhs[:, src_x * 128 : (src_x + 1) * 128] = probes_v[:, lax.div(at, 2)].reshape(768, 128)
-            q = recv[at_slot, 0:64, :]
-            o = recv[at_slot, 64:128, :]
-            held = half == lax.rem(at, 2)
-            for part, data in enumerate((q, o)):
-                pair = jnp.concatenate([data, data], axis=0)
-                cols = slice(part * 256, (part + 1) * 256)
-                rhs[src_x * 128 : (src_x + 1) * 128, cols] = jnp.where(
-                    held, pair, jnp.zeros_like(pair)
-                )
-            turned[at_slot] = jnp.concatenate([o, o], axis=0).T
-
+        for pair in range(2):
+            ats, qs, os = [], [], []
+            for src_x in (2 * pair, 2 * pair + 1):
+                shard = ((src_x // 2) * 2 + src_core) * 32 + src_z * 8 + (src_x % 2) * 4 + src_y
+                at_slot = slot(plane, src_core, src_x)
+                q, o = recv[at_slot, 0:64, :], recv[at_slot, 64:128, :]
+                q, o = (jnp.concatenate([part, part], axis=0) for part in (q, o))
+                turned[at_slot] = o.T
+                ats.append(block[shard])
+                qs.append(q)
+                os.append(o)
+            side = lax.rem(ats[0], 2)
+            one, two = (probes_v[:, lax.div(at, 2)].reshape(768, 128) for at in ats)
+            swapped = pltpu.roll(two, 64, axis=1)
+            two = jnp.where(lane_half * 0 + side == lax.rem(ats[1], 2), swapped, two)
+            rows = slice(at_half * 256 + pair * 128, at_half * 256 + (pair + 1) * 128)
+            lhs[:, rows] = jnp.where(lane_half == side, one, two)
+            rhs[rows, 0:256] = jnp.where(half == side, *qs)
+            rhs[rows, 256:512] = jnp.where(half == side, *os)
+
+    def accumulate():
         @pl.loop(0, 3)
         def _(m):
             rows = pl.ds(pl.multiple_of(m * 256, 256), 256)
@@ -193,6 +192,12 @@
 
     @pl.loop(0, ROUNDS + LAG_D)
     def _(t):
+        @pl.when((t >= 1) & (t + AHEAD < ROUNDS))
+        def _():
+            stage(t + AHEAD)
+            far(t + AHEAD).start()
+            near(t + AHEAD).start()
+
         @pl.when((t >= 1) & (t < ROUNDS - DIRECT))
         def _():
             far(t).wait_recv()
@@ -218,12 +223,15 @@
                 for i in range(8):
                     load_probes(i).wait()
 
-            compute(t - LAG_X, core)
-
         @pl.when(t >= LAG_D)
         def _():
             across(t - LAG_D).wait_recv()
-            compute(t - LAG_D, 1 - core)
+            arrange(t - LAG_D, 1 - core, 1)
+            accumulate()
+
+        @pl.when((t >= LAG_X) & (t < ROUNDS + LAG_X))
+        def _():
+            arrange(t - LAG_X, core, 0)
 
     @pl.loop(0, ROUNDS)
     def _(k):

time: 71.2 us -> 67.2 us (0.944)
  Pallas kernels: 70.4 us -> 66.5 us
    pallas_call x1, Pallas kernels: 66 us -> 62.1 us  [per_device(): pl.pallas_call(move_kernel, out_shape=(pltpu.VMEM((128, 128, 256), BF16),...]
where the time goes in v3:
time: 67.2 us; the launch traced here: 67.1 us
  Pallas kernels  66.5 us (99%)
    pallas_call x1, Pallas kernels, per_device(): pl.pallas_call(move_kernel, out_shape=(pltpu.VMEM((128, 128, 256), BF16),...  62.1 us
    pallas_call x1, Pallas kernels, per_device(): pl.pallas_call(place_kernel, out_shape=(jax.ShapeDtypeStruct((8192, 256),...  4.36 us

profile of v3, /device:TPU:1, one launch (start us, length us, event | category | flops | bytes accessed | tf_op | source)
XLA Modules:
  0.0 67.1 jit_solution(8717628696993931037)
XLA Ops:
  0.6 62.1 %move.1 = (bf16[128,128,256]{2,1,0:T(8,128)(2,1)S(1)}, bf16[128,256,128]{2,1,0:T(8,128)(2,1)S(1)}, f32[768,512]{1,0:T(8,128)S(1)}, s32[1,128]{1,0:T(1,128)S(1)}) custom-call(s32[32]{0:T(128)} %owner.1, s32[128]{0:T(128)} %block.1, s32[1,128]{1,0:T(1,128)} %bitcast.19, f32[8,32,2,8,128]{4,3,2,1,0:T(8,128)} %bitcast.17, f32[8,32,2,8,128]{4,3,2,1,0:T(8,128)} %bitcast.18, ...), custom_call_target="tpu_custom_call" | custom-call | tf_op jit(solution)/shard_map/move/pallas_call | solution.py:294
  62.8 4.4 %place.1 = (bf16[8192,256]{1,0:T(8,128)(2,1)}, bf16[256,8192]{1,0:T(8,128)(2,1)}, f32[768,256]{1,0:T(8,128)}, f32[256,768]{1,0:T(8,128)}) custom-call(s32[1,128]{1,0:T(1,128)S(1)} %get-tuple-element.12.slot_of, bf16[128,128,256]{2,1,0:T(8,128)(2,1)S(1)} %get-tuple-element.13.recv, bf16[128,256,128]{2,1,0:T(8,128)(2,1)S(1)} %get-tuple-element.14.turned, ...), custom_call_target="tpu_custom_call" | custom-call | tf_op jit(solution)/shard_map/place/pallas_call | solution.py:327

commit v4 on v3

--- a/solution.py
+++ b/solution.py
@@ -12,7 +12,6 @@
 ROUNDS = 16
 LAG_X = 3
 LAG_D = 4
-DIRECT = 0
 AHEAD = 4
 
 
@@ -37,18 +36,16 @@
 
 
 def move_kernel(
-    owner, block, block_row, query, output, probes,
+    owner_hbm, block_hbm, query, output, probes,
     recv, turned, prints, slot_of,
-    query_f, output_f, probes_v, staged, relay, lhs, rhs,
-    load_sem, probe_sem, near_s, near_r, far_s, far_r, x_s, x_r, d_s, d_r,
+    owner, block, block_row, slot_row, query_f, output_f, probes_v, staged, relay, lhs, rhs,
+    level, map_sem, load_sem, probe_sem, near_s, near_r, far_s, far_r, x_s, x_r, d_s, d_r,
 ):
     x, y, z, core = place()
     mine = z * 4 + y
     barrier = pltpu.get_barrier_semaphore()
-    peers = [device(x, y + k % 4, z + k // 4, core) for k in range(1, ROUNDS)]
-    peers += [device(x + d, y, z, core) for d in (1, 2, 3)] + [device(x, y, z, 1 - core)]
-    if DIRECT:
-        peers += [device(x + d, y + 2, z + 2, core) for d in (1, 2, 3)]
+    beside = [device(x, y + dy, z + dz, core) for dy, dz in ((1, 0), (3, 0), (0, 1), (0, 3))]
+    peers = [device(x + d, y, z, core) for d in (1, 2, 3)] + [device(x, y, z, 1 - core)] + beside
 
     def load(kind, i):
         src, dst = ((query, query_f), (output, output_f))[kind]
@@ -58,6 +55,13 @@
         rows = pl.ds(i * 12, 12)
         return pltpu.make_async_copy(probes.at[rows], probes_v.at[rows], probe_sem.at[i])
 
+    maps = [
+        pltpu.make_async_copy(owner_hbm, owner, map_sem.at[0]),
+        pltpu.make_async_copy(block_hbm, block, map_sem.at[1]),
+        pltpu.make_async_copy(block_hbm, block_row, map_sem.at[2]),
+    ]
+    for copy in maps:
+        copy.start()
     for i in range(8):
         load(0, i).start()
         load(1, i).start()
@@ -95,14 +99,6 @@
             remote(own, own, x_s.at[k, 2], x_r.at[k, 2], device(x + 2, y, z, core)),
         )
 
-    def diagonal():
-        k, own = ROUNDS - 1, recv.at[slot(mine, core, x)]
-        return [
-            remote(staged.at[k, other], own, x_s.at[k, i], x_r.at[k, i],
-                   device(x + d, y + 2, z + 2, core))
-            for i, (d, other) in enumerate(((1, 1), (3, 1), (2, 0)))
-        ]
-
     def across(k):
         half = recv.at[pl.ds(slot(plane_of(k), core, 0), 4)]
         return remote(half, half, d_s.at[k], d_r.at[k], device(x, y, z, 1 - core))
@@ -122,27 +118,35 @@
         for other in (0, 1):
             cut(staged.at[k, other], k, other)
 
+    def send(k):
+        far(k).start()
+        near(k).start()
+
+    def pass_on(i):
+        for peer in beside:
+            pl.semaphore_signal(level.at[i], 1, device_id=peer, device_id_type=MESH)
+
+    for copy in maps:
+        copy.wait()
     for i in range(8):
         load(0, i).wait()
         load(1, i).wait()
     cut(recv.at[slot(mine, core, x)], 0, 0)
     cut(relay.at[0], 0, 1)
-    if DIRECT:
-        stage(ROUNDS - 1)
     stage(1)
     pl.semaphore_wait(barrier, len(peers))
     for copy in along(0):
         copy.start()
-    far(1).start()
-    near(1).start()
-    if DIRECT:
-        for copy in diagonal():
-            copy.start()
-    for k in range(2, AHEAD + 1):
-        stage(k)
-        far(k).start()
-        near(k).start()
-
+    send(1)
+    pass_on(0)
+    stage(2)
+    send(2)
+    stage(4)
+    send(4)
+    stage(3)
+    pl.semaphore_wait(level.at[0], 4)
+    pass_on(1)
+    send(3)
     for i in range(8):
         load_probes(i).start()
     prints[...] = jnp.zeros_like(prints)
@@ -153,9 +157,11 @@
     src_x = lax.div(rep, 2) * 2 + lax.rem(lax.div(tp, 4), 2)
     where = slot(lax.div(tp, 8) * 4 + lax.rem(tp, 4), lax.rem(rep, 2), src_x)
     hit = held_block == lax.broadcasted_iota(jnp.int32, (128, 128), 1).astype(F32)
-    slot_of[...] = jnp.sum(
+    slot_row[...] = jnp.sum(
         jnp.where(hit, where.astype(F32), 0.0), axis=0, keepdims=True
     ).astype(jnp.int32)
+    to_scalar = pltpu.make_async_copy(slot_row, slot_of, map_sem.at[0])
+    to_scalar.start()
 
     half = lax.div(lax.broadcasted_iota(jnp.int32, (128, 256), 0), 64)
 
@@ -172,7 +178,7 @@
                 q, o = recv[at_slot, 0:64, :], recv[at_slot, 64:128, :]
                 q, o = (jnp.concatenate([part, part], axis=0) for part in (q, o))
                 turned[at_slot] = o.T
-                ats.append(block[shard])
+                ats.append(block[0, shard])
                 qs.append(q)
                 os.append(o)
             side = lax.rem(ats[0], 2)
@@ -195,10 +201,19 @@
         @pl.when((t >= 1) & (t + AHEAD < ROUNDS))
         def _():
             stage(t + AHEAD)
-            far(t + AHEAD).start()
-            near(t + AHEAD).start()
-
-        @pl.when((t >= 1) & (t < ROUNDS - DIRECT))
+
+            @pl.when(t + AHEAD == 7)
+            def _():
+                pl.semaphore_wait(level.at[1], 4)
+                pass_on(2)
+
+            @pl.when(t + AHEAD == 15)
+            def _():
+                pl.semaphore_wait(level.at[2], 4)
+
+            send(t + AHEAD)
+
+        @pl.when((t >= 1) & (t < ROUNDS))
         def _():
             far(t).wait_recv()
             first, second, third = along(t)
@@ -207,11 +222,6 @@
             near(t).wait_recv()
             third.start()
 
-        if DIRECT:
-            @pl.when(t == ROUNDS - 1)
-            def _():
-                near(t).wait_recv()
-
         @pl.when((t >= LAG_X) & (t < ROUNDS + LAG_X))
         def _():
             for copy in along(t - LAG_X):
@@ -233,14 +243,13 @@
         def _():
             arrange(t - LAG_X, core, 0)
 
+    to_scalar.wait()
+
     @pl.loop(0, ROUNDS)
     def _(k):
         @pl.when(k >= 1)
         def _():
             near(k).wait_send()
-
-        @pl.when((k >= 1) & (k < ROUNDS - DIRECT))
-        def _():
             far(k).wait_send()
 
         for copy in along(k):
@@ -297,11 +306,15 @@
             pltpu.VMEM((128, 128, 256), BF16),
             pltpu.VMEM((128, 256, 128), BF16),
             pltpu.VMEM((768, 512), F32),
+            pltpu.SMEM((1, 128), jnp.int32),
+        ),
+        in_specs=[hbm, hbm, hbm, hbm, hbm],
+        out_specs=(vmem, vmem, vmem, smem),
+        scratch_shapes=[
+            pltpu.SMEM((32,), jnp.int32),
+            pltpu.SMEM((1, 128), jnp.int32),
             pltpu.VMEM((1, 128), jnp.int32),
-        ),
-        in_specs=[smem, smem, vmem, hbm, hbm, hbm],
-        out_specs=(vmem, vmem, vmem, vmem),
-        scratch_shapes=[
+            pltpu.VMEM((1, 128), jnp.int32),
             pltpu.VMEM((8, 32, 2, 8, 128), F32),
             pltpu.VMEM((8, 32, 2, 8, 128), F32),
             pltpu.VMEM((96, 64, 8, 128), BF16),
@@ -309,7 +322,7 @@
             pltpu.VMEM((ROUNDS, 128, 256), BF16),
             pltpu.VMEM((768, 512), BF16),
             pltpu.VMEM((512, 512), BF16),
-            dma((2, 8)), dma((8,)), dma((ROUNDS,)), dma((ROUNDS,)), dma((ROUNDS,)), dma((ROUNDS,)),
+            pltpu.SemaphoreType.REGULAR((3,)), dma((3,)), dma((2, 8)), dma((8,)), dma((ROUNDS,)), dma((ROUNDS,)), dma((ROUNDS,)), dma((ROUNDS,)),
             dma((ROUNDS, 3)), dma((ROUNDS, 3)), dma((ROUNDS,)), dma((ROUNDS,)),
         ],
         compiler_params=pltpu.CompilerParams(
@@ -318,7 +331,6 @@
         name="move",
     )(
         in_hbm(slice_owner),
-        in_hbm(shard_block),
         in_hbm(shard_block.reshape(1, 128)),
         in_hbm(tiles(trainer_query[0])),
         in_hbm(tiles(jnp.swapaxes(trainer_output, 1, 2)[0])),

time: 67.2 us -> 65.3 us (0.972)
  Pallas kernels: 66.5 us -> 64.6 us
    pallas_call x1, Pallas kernels: 62.1 us -> 60.7 us  [per_device(): pl.pallas_call(move_kernel, out_shape=(pltpu.VMEM((128, 128, 256), BF16),...]
where the time goes in v4:
time: 65.3 us; the launch traced here: 65.2 us
  Pallas kernels  64.6 us (99%)
    pallas_call x1, Pallas kernels, per_device(): pl.pallas_call(move_kernel, out_shape=(pltpu.VMEM((128, 128, 256), BF16),...  60.7 us
    pallas_call x1, Pallas kernels, per_device(): pl.pallas_call(place_kernel, out_shape=(jax.ShapeDtypeStruct((8192, 256),...  3.82 us

profile of v4, /device:TPU:1, one launch (start us, length us, event | category | flops | bytes accessed | tf_op | source)
XLA Modules:
  0.0 65.2 jit_solution(13260194491219085400)
XLA Ops:
  0.6 60.7 %move.1 = (bf16[128,128,256]{2,1,0:T(8,128)(2,1)S(1)}, bf16[128,256,128]{2,1,0:T(8,128)(2,1)S(1)}, f32[768,512]{1,0:T(8,128)S(1)}, s32[1,128]{1,0:T(1,128)S(4)}) custom-call(s32[32]{0:T(128)} %owner_hbm.1, s32[1,128]{1,0:T(1,128)} %bitcast.19, f32[8,32,2,8,128]{4,3,2,1,0:T(8,128)} %bitcast.17, f32[8,32,2,8,128]{4,3,2,1,0:T(8,128)} %bitcast.18, ...), custom_call_target="tpu_custom_call" | custom-call | tf_op jit(solution)/shard_map/move/pallas_call | solution.py:303
  61.4 3.8 %place.1 = (bf16[8192,256]{1,0:T(8,128)(2,1)}, bf16[256,8192]{1,0:T(8,128)(2,1)}, f32[768,256]{1,0:T(8,128)}, f32[256,768]{1,0:T(8,128)}) custom-call(s32[1,128]{1,0:T(1,128)S(4)} %get-tuple-element.12.slot_of, bf16[128,128,256]{2,1,0:T(8,128)(2,1)S(1)} %get-tuple-element.13.recv, bf16[128,256,128]{2,1,0:T(8,128)(2,1)S(1)} %get-tuple-element.14.turned, ...), custom_call_target="tpu_custom_call" | custom-call | tf_op jit(solution)/shard_map/place/pallas_call | solution.py:339

commit v5 on v4

--- a/solution.py
+++ b/solution.py
@@ -12,16 +12,21 @@
 ROUNDS = 16
 LAG_X = 3
 LAG_D = 4
-AHEAD = 4
-
-
-def near_first(i):
-    return lax.rem(lax.div(i * (i + 1), 2), 4)
+AHEAD = 6
+
+
+STEPS = (
+    (0, 0), (1, 0), (0, 1), (3, 0), (0, 3), (1, 1), (3, 3), (2, 0),
+    (1, 3), (3, 1), (0, 2), (2, 1), (1, 2), (2, 3), (3, 2), (2, 2),
+)
 
 
 def offset_of(k):
     k = jnp.int32(k)
-    return near_first(lax.rem(k, 4)), near_first(lax.div(k, 4))
+    return tuple(
+        sum(steps[i] * (k == n).astype(jnp.int32) for n, steps in enumerate(STEPS) if steps[i])
+        for i in (0, 1)
+    )
 
 
 def place():
@@ -47,6 +52,9 @@
     beside = [device(x, y + dy, z + dz, core) for dy, dz in ((1, 0), (3, 0), (0, 1), (0, 3))]
     peers = [device(x + d, y, z, core) for d in (1, 2, 3)] + [device(x, y, z, 1 - core)] + beside
 
+    for peer in peers:
+        pl.semaphore_signal(barrier, 1, device_id=peer, device_id_type=MESH)
+
     def load(kind, i):
         src, dst = ((query, query_f), (output, output_f))[kind]
         return pltpu.make_async_copy(src.at[i], dst.at[i], load_sem.at[kind, i])
@@ -65,9 +73,6 @@
     for i in range(8):
         load(0, i).start()
         load(1, i).start()
-    for peer in peers:
-        pl.semaphore_signal(barrier, 1, device_id=peer, device_id_type=MESH)
-
     def remote(src, dst, send, receive, target):
         return pltpu.make_async_remote_copy(
             src_ref=src, dst_ref=dst, send_sem=send, recv_sem=receive,
@@ -139,14 +144,13 @@
         copy.start()
     send(1)
     pass_on(0)
-    stage(2)
-    send(2)
-    stage(4)
-    send(4)
-    stage(3)
-    pl.semaphore_wait(level.at[0], 4)
-    pass_on(1)
-    send(3)
+    for k in range(2, AHEAD + 1):
+        stage(k)
+        if k == 5:
+            pl.semaphore_wait(level.at[0], 4)
+            pass_on(1)
+        send(k)
+
     for i in range(8):
         load_probes(i).start()
     prints[...] = jnp.zeros_like(prints)
@@ -191,10 +195,15 @@
             rhs[rows, 256:512] = jnp.where(half == side, *os)
 
     def accumulate():
-        @pl.loop(0, 3)
+        @pl.loop(0, 2)
         def _(m):
-            rows = pl.ds(pl.multiple_of(m * 256, 256), 256)
+            rows = pl.ds(pl.multiple_of(m * 384, 384), 384)
             prints[rows, :] += jnp.dot(lhs[rows, :], rhs[...], preferred_element_type=F32)
+
+    def turn(t):
+        y_swap, z_swap = ((at == 0).astype(jnp.int32) * 2 for at in (y, z))
+        first, second, third, fourth = ((t == n).astype(jnp.int32) for n in (1, 2, 3, 4))
+        return t + y_swap * (first - third) + z_swap * (second - fourth)
 
     @pl.loop(0, ROUNDS + LAG_D)
     def _(t):
@@ -202,7 +211,13 @@
         def _():
             stage(t + AHEAD)
 
-            @pl.when(t + AHEAD == 7)
+            if AHEAD < 5:
+                @pl.when(t + AHEAD == 5)
+                def _():
+                    pl.semaphore_wait(level.at[0], 4)
+                    pass_on(1)
+
+            @pl.when(t + AHEAD == 11)
             def _():
                 pl.semaphore_wait(level.at[1], 4)
                 pass_on(2)
@@ -215,18 +230,19 @@
 
         @pl.when((t >= 1) & (t < ROUNDS))
         def _():
-            far(t).wait_recv()
-            first, second, third = along(t)
+            k = turn(t)
+            far(k).wait_recv()
+            first, second, third = along(k)
             first.start()
             second.start()
-            near(t).wait_recv()
+            near(k).wait_recv()
             third.start()
 
         @pl.when((t >= LAG_X) & (t < ROUNDS + LAG_X))
         def _():
-            for copy in along(t - LAG_X):
+            for copy in along(turn(t - LAG_X)):
                 copy.wait_recv()
-            across(t - LAG_X).start()
+            across(turn(t - LAG_X)).start()
 
             @pl.when(t == LAG_X)
             def _():
@@ -235,13 +251,13 @@
 
         @pl.when(t >= LAG_D)
         def _():
-            across(t - LAG_D).wait_recv()
-            arrange(t - LAG_D, 1 - core, 1)
+            across(turn(t - LAG_D)).wait_recv()
+            arrange(turn(t - LAG_D), 1 - core, 1)
             accumulate()
 
         @pl.when((t >= LAG_X) & (t < ROUNDS + LAG_X))
         def _():
-            arrange(t - LAG_X, core, 0)
+            arrange(turn(t - LAG_X), core, 0)
 
     to_scalar.wait()
 

time: 65.3 us -> 63.6 us (0.974)
  Pallas kernels: 64.6 us -> 62.9 us
    pallas_call x1, Pallas kernels: 60.7 us -> 59.1 us  [per_device(): pl.pallas_call(move_kernel, out_shape=(pltpu.VMEM((128, 128, 256), BF16),...]
where the time goes in v5:
time: 63.6 us; the launch traced here: 63.5 us
  Pallas kernels  62.9 us (99%)
  between operations  0.64 us (1%)
    pallas_call x1, Pallas kernels, per_device(): pl.pallas_call(move_kernel, out_shape=(pltpu.VMEM((128, 128, 256), BF16),...  59.1 us
    pallas_call x1, Pallas kernels, per_device(): pl.pallas_call(place_kernel, out_shape=(jax.ShapeDtypeStruct((8192, 256),...  3.82 us

profile of v5, /device:TPU:1, one launch (start us, length us, event | category | flops | bytes accessed | tf_op | source)
XLA Modules:
  0.0 63.5 jit_solution(3756970150219370135)
XLA Ops:
  0.6 59.1 %move.1 = (bf16[128,128,256]{2,1,0:T(8,128)(2,1)S(1)}, bf16[128,256,128]{2,1,0:T(8,128)(2,1)S(1)}, f32[768,512]{1,0:T(8,128)S(1)}, s32[1,128]{1,0:T(1,128)S(4)}) custom-call(s32[32]{0:T(128)} %owner_hbm.1, s32[1,128]{1,0:T(1,128)} %bitcast.19, f32[8,32,2,8,128]{4,3,2,1,0:T(8,128)} %bitcast.17, f32[8,32,2,8,128]{4,3,2,1,0:T(8,128)} %bitcast.18, ...), custom_call_target="tpu_custom_call" | custom-call | tf_op jit(solution)/shard_map/move/pallas_call | solution.py:319
  59.7 3.8 %place.1 = (bf16[8192,256]{1,0:T(8,128)(2,1)}, bf16[256,8192]{1,0:T(8,128)(2,1)}, f32[768,256]{1,0:T(8,128)}, f32[256,768]{1,0:T(8,128)}) custom-call(s32[1,128]{1,0:T(1,128)S(4)} %get-tuple-element.12.slot_of, bf16[128,128,256]{2,1,0:T(8,128)(2,1)S(1)} %get-tuple-element.13.recv, bf16[128,256,128]{2,1,0:T(8,128)(2,1)S(1)} %get-tuple-element.14.turned, ...), custom_call_target="tpu_custom_call" | custom-call | tf_op jit(solution)/shard_map/place/pallas_call | solution.py:355

commit v6 on v5

--- a/solution.py
+++ b/solution.py
@@ -195,10 +195,7 @@
             rhs[rows, 256:512] = jnp.where(half == side, *os)
 
     def accumulate():
-        @pl.loop(0, 2)
-        def _(m):
-            rows = pl.ds(pl.multiple_of(m * 384, 384), 384)
-            prints[rows, :] += jnp.dot(lhs[rows, :], rhs[...], preferred_element_type=F32)
+        prints[...] += jnp.dot(lhs[...], rhs[...], preferred_element_type=F32)
 
     def turn(t):
         y_swap, z_swap = ((at == 0).astype(jnp.int32) * 2 for at in (y, z))

time: 63.6 us -> 63.2 us (level)
  no operation moved by 1% of the time
where the time goes in v6:
time: 63.2 us; the launch traced here: 63.1 us
  Pallas kernels  62.5 us (99%)
  between operations  0.64 us (1%)
    pallas_call x1, Pallas kernels, per_device(): pl.pallas_call(move_kernel, out_shape=(pltpu.VMEM((128, 128, 256), BF16),...  58.6 us
    pallas_call x1, Pallas kernels, per_device(): pl.pallas_call(place_kernel, out_shape=(jax.ShapeDtypeStruct((8192, 256),...  3.82 us

profile of v6, /device:TPU:1, one launch (start us, length us, event | category | flops | bytes accessed | tf_op | source)
XLA Modules:
  0.0 63.1 jit_solution(13921686947115662425)
XLA Ops:
  0.6 58.6 %move.1 = (bf16[128,128,256]{2,1,0:T(8,128)(2,1)S(1)}, bf16[128,256,128]{2,1,0:T(8,128)(2,1)S(1)}, f32[768,512]{1,0:T(8,128)S(1)}, s32[1,128]{1,0:T(1,128)S(4)}) custom-call(s32[32]{0:T(128)} %owner_hbm.1, s32[1,128]{1,0:T(1,128)} %bitcast.19, f32[8,32,2,8,128]{4,3,2,1,0:T(8,128)} %bitcast.17, f32[8,32,2,8,128]{4,3,2,1,0:T(8,128)} %bitcast.18, ...), custom_call_target="tpu_custom_call" | custom-call | tf_op jit(solution)/shard_map/move/pallas_call | solution.py:316
  59.3 3.8 %place.1 = (bf16[8192,256]{1,0:T(8,128)(2,1)}, bf16[256,8192]{1,0:T(8,128)(2,1)}, f32[768,256]{1,0:T(8,128)}, f32[256,768]{1,0:T(8,128)}) custom-call(s32[1,128]{1,0:T(1,128)S(4)} %get-tuple-element.12.slot_of, bf16[128,128,256]{2,1,0:T(8,128)(2,1)S(1)} %get-tuple-element.13.recv, bf16[128,256,128]{2,1,0:T(8,128)(2,1)S(1)} %get-tuple-element.14.turned, ...), custom_call_target="tpu_custom_call" | custom-call | tf_op jit(solution)/shard_map/place/pallas_call | solution.py:352
